TPU v7x, 32 devices: a whole 2x2x4 slice. The times are simulated.
32 devices in a mesh: gx: 8 (over z, x), gy: 4 (over y, core).
Axes of the slice: x: 2, y: 2, z: 4, core: 2. Of those that a mesh axis runs over, the one named last changes fastest.
Arguments:
- orbitals: bfloat16 [20000, 200], P('gx'), may hold values from -6 to 6
- projector: bfloat16 [6016, 20000], P('gy', 'gx'), may hold values from -0.0390625 to 0.0390625
- integrals: bfloat16 [8, 6016, 6016], P('gx', 'gy'), may hold values from -1 to 1
Outputs:
- exchange_matrix: float32 [6016, 6016], P('gx', 'gy')
- exchange_orbitals: float32 [20000, 200], P('gx', 'gy')
- energy_mean: float32 [], replicated
- trace_mean: float32 [], replicated
All inputs are finite; a program needn't handle non-finite values.
Results may differ from a plain program's by a relative error of at most 0.008.
Values may be sent and summed in bfloat16 or wider, within the bound.
No kernel may reach another device: no remote copies, remote signals or barrier semaphores. Data moves between devices by JAX's collectives and lax.ppermute only.
A program may use at most 128 MiB of HBM per device.

v0:
```python
import jax
import jax.numpy as jnp
from jax import lax
from jax.sharding import PartitionSpec as P


def spread(block, axis, holder):
    block = jnp.where(lax.axis_index(axis) == holder, block, jnp.zeros_like(block))
    return lax.psum(block, axis)


def on_device(orbitals, projector, integrals):
    part_rows = projector.shape[0]
    partial_value = jnp.dot(projector, orbitals, preferred_element_type=jnp.float32)
    own_admm = lax.psum(partial_value, "gx").astype(jnp.bfloat16)
    admm = lax.all_gather(own_admm, "gy", axis=0, tiled=True)
    half = lax.dot_general(
        integrals, admm, (((2,), (0,)), ((), ())), preferred_element_type=jnp.float32
    ).astype(jnp.bfloat16)
    size_x = lax.axis_size("gx")
    block_rows = admm.shape[0] // size_x
    index_x = lax.axis_index("gx")
    index_y = lax.axis_index("gy")
    all_half = lax.all_gather(half, "gx", axis=0, tiled=True)
    first_row = index_x * block_rows
    root = first_row // part_rows
    offset = jnp.clip(first_row - index_y * part_rows, 0, part_rows - block_rows)
    mine = lax.dynamic_slice_in_dim(all_half, offset, block_rows, 1)
    columns = spread(mine, "gy", root)
    exchange = lax.dot_general(
        columns, all_half, (((0, 2), (0, 2)), ((), ())), preferred_element_type=jnp.float32
    )
    row_ids = index_x * block_rows + lax.iota(jnp.int32, block_rows)
    col_ids = index_y * part_rows + lax.iota(jnp.int32, part_rows)
    diag_mask = row_ids[:, None] == col_ids[None, :]
    trace_part = jnp.sum(jnp.where(diag_mask, exchange, 0.0))
    trace_total = lax.psum(trace_part, ("gx", "gy"))
    admm_wide = admm.astype(jnp.float32)
    col_orbs = lax.dynamic_slice_in_dim(admm_wide, index_x * block_rows, block_rows, 0)
    row_orbs = lax.dynamic_slice_in_dim(admm_wide, index_y * part_rows, part_rows, 0)
    applied_part = lax.dot_general(
        exchange,
        col_orbs,
        (((0,), (0,)), ((), ())),
        precision=lax.Precision.HIGHEST,
        preferred_element_type=jnp.float32,
    )
    energy_part = jnp.sum(row_orbs * applied_part)
    energy_total = lax.psum(energy_part, ("gx", "gy"))
    applied = lax.psum(applied_part, "gx")
    applied_low = applied.astype(jnp.bfloat16)
    back_part = lax.dot_general(
        projector, applied_low, (((0,), (0,)), ((), ())), preferred_element_type=jnp.float32
    )
    back = lax.psum_scatter(back_part, "gy", scatter_dimension=1, tiled=True)
    total_adm = admm.shape[0]
    energy_mean = -0.5 * energy_total / (total_adm * admm.shape[1])
    trace_mean = trace_total / total_adm
    return (exchange, back, energy_mean, trace_mean)


def solution(mesh):
    return jax.shard_map(
        on_device,
        mesh=mesh,
        in_specs=(P("gx", None), P("gy", "gx"), P("gx", "gy", None)),
        out_specs=(P("gx", "gy"), P("gx", "gy"), P(), P()),
        check_vma=False,
    )
```

profile of v0, /device:TPU:12, one launch (start us, length us, event | category | flops | bytes accessed | tf_op | source)
XLA Modules:
  0.0 447.2 jit_solution(2069144303628339878)
XLA Ops:
  7.2 0.0 copy-start
  7.2 0.0 all-gather.6.cloned.1.call-start
  7.2 1.2 copy-done
  8.4 4.9 %fusion.13 = f32[1504,200]{0,1:T(8,128)S(1)} fusion(bf16[1504,2500]{0,1:T(8,128)(2,1)} %param.4, bf16[2500,200]{0,1:T(8,128)(2,1)S(1)} %copy-done), kind=kOutput, calls=%fused_computation.17 | convolution fusion | flops 1504000000 | bytes 9723200 | tf_op jit(solution)/shard_map/dot_general | solution.py:14
  13.3 72.9 %all-reduce.8 = bf16[1504,200]{0,1:T(8,128)(2,1)} all-reduce(f32[1504,200]{0,1:T(8,128)S(1)} %fusion.13), channel_id=1, replica_groups=mesh['gx'=8,'gy'=4] {'gx'}, use_global_device_ids=true, to_apply=%region_0.0 | all-reduce | flops 300800 | bytes 1804800 | tf_op jit(solution)/shard_map/psum | solution.py:15
  86.2 0.0 all-gather.6.cloned.1.call-update
  86.2 0.0 all-gather.8.cloned.1.call-start
  86.3 23.8 %all-gather.6.cloned.1.call-done = bf16[4,1504,200]{1,2,0:T(8,128)(2,1)} async-done(((bf16[1,1504,200]{1,2,0:T(8,128)(2,1)}), bf16[4,1504,200]{1,2,0:T(8,128)(2,1)}) %all-gather.6.cloned.1.call-update) | async-done | bytes 2406416 | tf_op jit(solution)/shard_map/all_gather | solution.py:16
  110.1 3.0 copy.8
  113.1 4.4 reshape.24
  117.5 13.3 %fusion.6 = bf16[1,1504,200]{1,2,0:T(8,128)(2,1)} fusion(bf16[6016,200]{0,1:T(8,128)(2,1)} %reshape.24, bf16[1,1504,6016]{2,1,0:T(8,128)(2,1)} %param.5), kind=kOutput, calls=%fused_computation.7 | convolution fusion | flops 3619526400 | bytes 21104128 | tf_op jit(solution)/shard_map/dot_general | solution.py:17
  130.8 0.0 all-gather.8.cloned.1.call-update
  130.8 0.2 all-reduce.7.cloned.1.call-start
  131.1 81.9 %all-gather.8.cloned.1.call-done = bf16[8,1504,200]{1,2,0:T(8,128)(2,1)} async-done(((bf16[1,1504,200]{1,2,0:T(8,128)(2,1)}), bf16[8,1504,200]{1,2,0:T(8,128)(2,1)}) %all-gather.8.cloned.1.call-update) | async-done | bytes 4812816 | tf_op jit(solution)/shard_map/all_gather | solution.py:24
  213.0 4.8 %dynamic-slice_select_fusion = bf16[8,752,200]{1,2,0:T(8,128)(2,1)} fusion(bf16[8,1504,200]{1,2,0:T(8,128)(2,1)} %all-gather.8.cloned.1.call-done, s32[]{:T(128)S(6)} %min.4, pred[]{:T(512)S(6)} %eq.16), kind=kLoop, calls=%fused_computation.6 | loop fusion | flops 1203200 | bytes 4812805 | tf_op jit(solution)/shard_map/jit(_where)/select_n | solution.py:8
  217.8 0.0 all-reduce.7.cloned.1.call-update
  217.9 55.5 %all-reduce.7.cloned.1.call-done = bf16[8,752,200]{1,2,0:T(8,128)(2,1)} async-done(((bf16[8,752,200]{1,2,0:T(8,128)(2,1)}), bf16[8,752,200]{1,2,0:T(8,128)(2,1)}) %all-reduce.7.cloned.1.call-update) | async-done | bytes 2406416 | tf_op jit(solution)/shard_map/psum | solution.py:9
  273.4 8.1 %select_reduce_fusion = (f32[]{:T(128)}, f32[752,1504]{1,0:T(8,128)S(1)}) fusion(s32[1504]{0:T(1024)S(1)} %iota_add_fusion, s32[752]{0:T(1024)S(1)} %iota_add_fusion.1, bf16[8,752,200]{1,2,0:T(8,128)(2,1)} %all-reduce.7.cloned.1.call-done, bf16[8,1504,200]{1,2,0:T(8,128)(2,1)} %all-gather.8.cloned.1.call-done), kind=kOutput, calls=%fused_computation.2 | convolution fusion | flops 3622618624 | bytes 11752260 | tf_op jit(solution)/shard_map/dot_general | solution.py:30
  281.5 0.0 copy-start.1
  281.5 5.0 %multiply_reduce_fusion = (f32[]{:T(128)}, f32[1504,200]{0,1:T(8,128)S(1)}) fusion(bf16[6016,200]{0,1:T(8,128)(2,1)} %reshape.24, s32[]{:T(128)S(6)} %select_n.28, f32[752,1504]{1,0:T(8,128)S(1)} %get-tuple-element.9, s32[]{:T(128)S(6)} %select_n.27), kind=kOutput, calls=%fused_computation.8 | convolution fusion | flops 2715321600 | bytes 6648844 | tf_op jit(solution)/shard_map/dot_general | solution.py:41
  286.6 0.0 copy-done.1
  286.6 72.6 %all-reduce.9 = bf16[1504,200]{0,1:T(8,128)(2,1)S(1)} all-reduce(f32[1504,200]{0,1:T(8,128)S(1)} %get-tuple-element.7), channel_id=1, replica_groups=mesh['gx'=8,'gy'=4] {'gx'}, use_global_device_ids=true, to_apply=%region_2.3 | all-reduce | flops 300800 | bytes 1804800 | tf_op jit(solution)/shard_map/psum | solution.py:50
  359.2 7.0 %convolution_bitcast_fusion = f32[2500,200]{0,1:T(8,128)} fusion(bf16[1504,2500]{0,1:T(8,128)(2,1)} %param.4, bf16[1504,200]{0,1:T(8,128)(2,1)S(1)} %all-reduce.9), kind=kOutput, calls=%fused_computation.3 | convolution fusion | flops 1504000000 | bytes 10121600 | tf_op jit(solution)/shard_map/dot_general | solution.py:52
  366.1 0.0 copy-start.2
  366.1 24.2 %fusion = f32[2500,56]{0,1:T(8,128)S(1)} fusion(f32[2500,200]{0,1:T(8,128)} %convolution_bitcast_fusion), kind=kCustom, calls=%all-reduce-scatter | all-reduce-scatter fusion | flops 560001 | bytes 2560512
  390.3 1.9 collective-permute-start
  392.2 0.0 copy-done.2
  392.3 0.6 dynamic-slice.5
  393.5 42.3 %all-reduce.2 = (f32[]{:T(128)}, f32[]{:T(128)}) all-reduce(f32[]{:T(128)} %get-tuple-element.6, f32[]{:T(128)} %get-tuple-element.8), channel_id=1, replica_groups=mesh['gx'=8,'gy'=4] {'gx','gy'}, use_global_device_ids=true, to_apply=%region_5.6 | all-reduce | flops 2 | bytes 16 | tf_op jit(solution)/shard_map/psum | solution.py:49
  437.1 0.0 collective-permute-done
  437.1 0.4 concatenate
  437.6 0.9 constant_dynamic-slice_fusion
  (3 shorter events, 0.0 us)
Async XLA Ops:
  7.2 1.2 copy-start
  7.2 102.9 %all-gather.6.cloned.1.call-start = ((), (), s32[]{:S(2)}) async-start(), calls=%async_computation.1 | async-start | bytes 3072000 | tf_op jit(solution)/shard_map/all_gather | solution.py:16
  86.2 126.8 %all-gather.8.cloned.1.call-start = ((), (), s32[]{:S(2)}) async-start(), calls=%async_computation.2 | async-start | bytes 5529600 | tf_op jit(solution)/shard_map/all_gather | solution.py:24
  130.8 142.6 %all-reduce.7.cloned.1.call-start = ((), (), s32[]{:S(2)}) async-start(), calls=%async_computation | async-start | bytes 4915200 | tf_op jit(solution)/shard_map/psum | solution.py:9
  281.5 5.0 %copy-start.1 = (f32[752,1504]{1,0:T(8,128)}, f32[752,1504]{1,0:T(8,128)S(1)}, u32[]{:S(2)}) copy-start(f32[752,1504]{1,0:T(8,128)S(1)} %get-tuple-element.9) | copy-start | bytes 13572100
  366.1 26.1 %copy-start.2 = (u32[32]{0:T(128)S(1)}, u32[32]{0:T(128)}, u32[]{:S(2)}) copy-start(u32[32]{0:T(128)} %constant.44) | copy-start | bytes 388
  390.3 46.8 %collective-permute-start = (f32[2500,18]{0,1:T(8,128)S(1)}, f32[2500,18]{0,1:T(8,128)S(1)}, u32[]{:S(2)}, u32[]{:S(2)}) collective-permute-start(f32[2500,18]{0,1:T(8,128)S(1)} %slice), channel_id=1, source_target_pairs={{0,1},{1,2},{2,3},{4,5},{5,6},{6,7},{8,9},{9,10},{10,11},{12,13},{... | collective-permute-start | bytes 540008
Sparse Core Ops, SparseCore 0:
  86.3 23.7 all-gather.5
  130.9 82.0 all-gather.7
  218.0 55.3 all-reduce.6
where the time goes:
time: 448 us; the launch traced here: 447 us
  blocking collectives  212 us (47%)
  waiting for transfers between devices  161 us (36%)
  matrix products  38.4 us (9%)
  between operations  18.1 us (4%)
  local copies, waits for them, and re-layouts  10.4 us (2%)
  other arithmetic  4.83 us (1%)
    all_gather x1, waiting for transfers between devices, on_device(): all_half = lax.all_gather(half, 'gx', axis=0, tiled=True)  81.9 us
    psum x1, blocking collectives, on_device(): own_admm = lax.psum(partial_value, 'gx').astype(jnp.bfloat16)  72.9 us
    psum x1, blocking collectives, on_device(): applied = lax.psum(applied_part, 'gx')  72.6 us
    psum x1, waiting for transfers between devices, spread(): return lax.psum(block, axis)  55.5 us
    psum x1, blocking collectives, on_device(): energy_total = lax.psum(energy_part, ('gx', 'gy'))  42.3 us
    unnamed x1, blocking collectives  24.2 us
    all_gather x1, waiting for transfers between devices, on_device(): admm = lax.all_gather(own_admm, 'gy', axis=0, tiled=True)  23.8 us
    dot_general x1, matrix products, on_device(): lax.dot_general(integrals, admm, (((2,), (0,)), ((), ())), preferred_elem...  13.3 us
  transfers between devices with their start and end apart: 4, of which 3 were waited for; matrix products, arithmetic and copies ran while one was open for 0% of the time, Pallas kernels for 0%

commit v1 on v0

--- a/solution.py
+++ b/solution.py
@@ -47,7 +47,9 @@
     )
     energy_part = jnp.sum(row_orbs * applied_part)
     energy_total = lax.psum(energy_part, ("gx", "gy"))
-    applied = lax.psum(applied_part, "gx")
+    applied = applied_part
+    for hop in (1, 2, 4):
+        applied = applied + lax.ppermute(applied, "gx", [(dev, dev ^ hop) for dev in range(8)])
     applied_low = applied.astype(jnp.bfloat16)
     back_part = lax.dot_general(
         projector, applied_low, (((0,), (0,)), ((), ())), preferred_element_type=jnp.float32

time: 448 us -> 488 us (1.089)
  waiting for transfers between devices: 161 us -> 267 us
  blocking collectives: 212 us -> 140 us
    ppermute x0 -> x3, waiting for transfers between devices: none -> 105 us  [on_device(): lax.ppermute(applied, 'gx', [(dev, dev ^ hop) for dev in range(8)])]
    psum x1 -> x0, blocking collectives: 72.6 us -> none  [on_device(): applied = lax.psum(applied_part, 'gx')]
  transfers between devices with their start and end apart: 4 -> 7, of which waited for: 3 -> 6; matrix products, arithmetic and copies ran while one was open for 0% -> 0% of each run, Pallas kernels for 0% -> 0%
where the time goes in v1:
time: 488 us; the launch traced here: 487 us
  waiting for transfers between devices  267 us (55%)
  blocking collectives  140 us (29%)
  matrix products  35.5 us (7%)
  between operations  18.1 us (4%)
  local copies, waits for them, and re-layouts  13.1 us (3%)
  other arithmetic  7.16 us (1%)
  starting transfers between devices  6.74 us (1%)
    ppermute x3, waiting for transfers between devices, on_device(): lax.ppermute(applied, 'gx', [(dev, dev ^ hop) for dev in range(8)])  105 us
    all_gather x1, waiting for transfers between devices, on_device(): all_half = lax.all_gather(half, 'gx', axis=0, tiled=True)  81.9 us
    psum x1, blocking collectives, on_device(): own_admm = lax.psum(partial_value, 'gx').astype(jnp.bfloat16)  72.9 us
    psum x1, waiting for transfers between devices, spread(): return lax.psum(block, axis)  55.5 us
    psum x1, blocking collectives, on_device(): energy_total = lax.psum(energy_part, ('gx', 'gy'))  42.4 us
    unnamed x1, blocking collectives  24.8 us
    all_gather x1, waiting for transfers between devices, on_device(): admm = lax.all_gather(own_admm, 'gy', axis=0, tiled=True)  23.8 us
    dot_general x1, matrix products, on_device(): lax.dot_general(integrals, admm, (((2,), (0,)), ((), ())), preferred_elem...  13.3 us
  transfers between devices with their start and end apart: 7, of which 6 were waited for; matrix products, arithmetic and copies ran while one was open for 0% of the time, Pallas kernels for 0%

profile of v1, /device:TPU:12, one launch (start us, length us, event | category | flops | bytes accessed | tf_op | source)
XLA Modules:
  0.0 487.2 jit_solution(8584397555581029447)
XLA Ops:
  7.2 0.0 copy-start
  7.2 0.0 all-gather.6.cloned.1.call-start
  7.2 1.2 copy-done
  8.4 4.9 %fusion.12 = f32[1504,200]{0,1:T(8,128)S(1)} fusion(bf16[1504,2500]{0,1:T(8,128)(2,1)} %param.4, bf16[2500,200]{0,1:T(8,128)(2,1)S(1)} %copy-done), kind=kOutput, calls=%fused_computation.17 | convolution fusion | flops 1504000000 | bytes 9723200 | tf_op jit(solution)/shard_map/dot_general | solution.py:14
  13.3 72.9 %all-reduce.7 = bf16[1504,200]{0,1:T(8,128)(2,1)} all-reduce(f32[1504,200]{0,1:T(8,128)S(1)} %fusion.12), channel_id=1, replica_groups=mesh['gx'=8,'gy'=4] {'gx'}, use_global_device_ids=true, to_apply=%region_0.0 | all-reduce | flops 300800 | bytes 1804800 | tf_op jit(solution)/shard_map/psum | solution.py:15
  86.2 0.0 all-gather.6.cloned.1.call-update
  86.2 0.0 all-gather.8.cloned.1.call-start
  86.3 23.8 %all-gather.6.cloned.1.call-done = bf16[4,1504,200]{1,2,0:T(8,128)(2,1)} async-done(((bf16[1,1504,200]{1,2,0:T(8,128)(2,1)}), bf16[4,1504,200]{1,2,0:T(8,128)(2,1)}) %all-gather.6.cloned.1.call-update) | async-done | bytes 2406416 | tf_op jit(solution)/shard_map/all_gather | solution.py:16
  110.1 3.0 copy.8
  113.1 4.4 reshape.24
  117.5 13.3 %fusion.6 = bf16[1,1504,200]{1,2,0:T(8,128)(2,1)} fusion(bf16[6016,200]{0,1:T(8,128)(2,1)} %reshape.24, bf16[1,1504,6016]{2,1,0:T(8,128)(2,1)} %param.5), kind=kOutput, calls=%fused_computation.7 | convolution fusion | flops 3619526400 | bytes 21104128 | tf_op jit(solution)/shard_map/dot_general | solution.py:17
  130.8 0.0 all-gather.8.cloned.1.call-update
  130.8 0.2 all-reduce.6.cloned.1.call-start
  131.1 81.9 %all-gather.8.cloned.1.call-done = bf16[8,1504,200]{1,2,0:T(8,128)(2,1)} async-done(((bf16[1,1504,200]{1,2,0:T(8,128)(2,1)}), bf16[8,1504,200]{1,2,0:T(8,128)(2,1)}) %all-gather.8.cloned.1.call-update) | async-done | bytes 4812816 | tf_op jit(solution)/shard_map/all_gather | solution.py:24
  213.0 4.8 dynamic-slice_select_fusion
  217.8 0.0 all-reduce.6.cloned.1.call-update
  217.8 55.5 %all-reduce.6.cloned.1.call-done = bf16[8,752,200]{1,2,0:T(8,128)(2,1)} async-done(((bf16[8,752,200]{1,2,0:T(8,128)(2,1)}), bf16[8,752,200]{1,2,0:T(8,128)(2,1)}) %all-reduce.6.cloned.1.call-update) | async-done | bytes 2406416 | tf_op jit(solution)/shard_map/psum | solution.py:9
  273.4 8.1 %select_reduce_fusion = (f32[]{:T(128)}, f32[752,1504]{1,0:T(8,128)S(1)}) fusion(s32[1504]{0:T(1024)S(1)} %iota_add_fusion, s32[752]{0:T(1024)S(1)} %iota_add_fusion.1, bf16[8,752,200]{1,2,0:T(8,128)(2,1)} %all-reduce.6.cloned.1.call-done, bf16[8,1504,200]{1,2,0:T(8,128)(2,1)} %all-gather.8.cloned.1.call-done), kind=kOutput, calls=%fused_computation.2 | convolution fusion | flops 3622618624 | bytes 11752260 | tf_op jit(solution)/shard_map/dot_general | solution.py:30
  281.5 0.0 copy-start.1
  281.5 3.4 fusion.9
  284.9 0.0 copy-done.1
  285.0 1.5 collective-permute-start
  286.5 27.2 %collective-permute-done = f32[1504,200]{0,1:T(8,128)S(1)} collective-permute-done((f32[1504,200]{0,1:T(8,128)S(1)}, f32[1504,200]{0,1:T(8,128)S(1)}, u32[]{:S(2)}, u32[]{:S(2)}) %collective-permute-start) | collective-permute-done | bytes 1203232 | tf_op jit(solution)/shard_map/ppermute | solution.py:52
  313.7 2.2 multiply_reduce_fusion
  315.9 0.5 collective-permute-start.1
  316.4 27.3 %collective-permute-done.1 = f32[1504,200]{0,1:T(8,128)S(1)} collective-permute-done((f32[1504,200]{0,1:T(8,128)S(1)}, f32[1504,200]{0,1:T(8,128)S(1)}, u32[]{:S(2)}, u32[]{:S(2)}) %collective-permute-start.1) | collective-permute-done | bytes 1203232 | tf_op jit(solution)/shard_map/ppermute | solution.py:52
  343.7 0.1 add.49
  343.8 2.5 collective-permute-start.2
  346.3 50.8 %collective-permute-done.2 = f32[1504,200]{0,1:T(8,128)S(1)} collective-permute-done((f32[1504,200]{0,1:T(8,128)S(1)}, f32[1504,200]{0,1:T(8,128)S(1)}, u32[]{:S(2)}, u32[]{:S(2)}) %collective-permute-start.2) | collective-permute-done | bytes 1203232 | tf_op jit(solution)/shard_map/ppermute | solution.py:52
  397.1 5.7 %convolution_bitcast_fusion = f32[2500,200]{0,1:T(8,128)S(1)} fusion(bf16[1504,2500]{0,1:T(8,128)(2,1)} %param.4, f32[1504,200]{0,1:T(8,128)S(1)} %add.49, f32[1504,200]{0,1:T(8,128)S(1)} %collective-permute-done.2), kind=kOutput, calls=%fused_computation.3 | convolution fusion | flops 1504601600 | bytes 11926400 | tf_op jit(solution)/shard_map/dot_general | solution.py:54
  402.8 0.0 copy-start.2
  402.8 24.8 %fusion = f32[2500,56]{0,1:T(8,128)} fusion(f32[2500,200]{0,1:T(8,128)S(1)} %convolution_bitcast_fusion), kind=kCustom, calls=%all-reduce-scatter | all-reduce-scatter fusion | flops 560001 | bytes 2560512
  427.6 1.0 slice
  428.5 1.9 collective-permute-start.3
  430.5 0.0 copy-done.2
  430.5 0.6 dynamic-slice.5
  431.7 42.4 %all-reduce.2 = (f32[]{:T(128)}, f32[]{:T(128)}) all-reduce(f32[]{:T(128)} %get-tuple-element.6, f32[]{:T(128)} %get-tuple-element.8), channel_id=1, replica_groups=mesh['gx'=8,'gy'=4] {'gx','gy'}, use_global_device_ids=true, to_apply=%region_4.5 | all-reduce | flops 2 | bytes 16 | tf_op jit(solution)/shard_map/psum | solution.py:49
  475.4 0.0 collective-permute-done.3
  475.5 2.1 concatenate
  477.5 0.9 constant_dynamic-slice_fusion
  (2 shorter events, 0.0 us)
Async XLA Ops:
  7.2 1.2 copy-start
  7.2 102.9 %all-gather.6.cloned.1.call-start = ((), (), s32[]{:S(2)}) async-start(), calls=%async_computation.1 | async-start | bytes 3072000 | tf_op jit(solution)/shard_map/all_gather | solution.py:16
  86.2 126.8 %all-gather.8.cloned.1.call-start = ((), (), s32[]{:S(2)}) async-start(), calls=%async_computation.2 | async-start | bytes 5529600 | tf_op jit(solution)/shard_map/all_gather | solution.py:24
  130.8 142.6 %all-reduce.6.cloned.1.call-start = ((), (), s32[]{:S(2)}) async-start(), calls=%async_computation | async-start | bytes 4915200 | tf_op jit(solution)/shard_map/psum | solution.py:9
  281.5 3.4 copy-start.1
  285.0 28.8 %collective-permute-start = (f32[1504,200]{0,1:T(8,128)S(1)}, f32[1504,200]{0,1:T(8,128)S(1)}, u32[]{:S(2)}, u32[]{:S(2)}) collective-permute-start(f32[1504,200]{0,1:T(8,128)S(1)} %fusion.9), channel_id=1, source_target_pairs={{0,4},{4,0},{8,12},{12,8},{16,20},{20,16},{24,28},{28,24},{1,5},{5... | collective-permute-start | bytes 3609608 | tf_op jit(solution)/shard_map/ppermute | solution.py:52
  315.9 27.8 %collective-permute-start.1 = (f32[1504,200]{0,1:T(8,128)S(1)}, f32[1504,200]{0,1:T(8,128)S(1)}, u32[]{:S(2)}, u32[]{:S(2)}) collective-permute-start(f32[1504,200]{0,1:T(8,128)S(1)} %get-tuple-element.7), channel_id=1, source_target_pairs={{0,8},{4,12},{8,0},{12,4},{16,24},{20,28},{24,16},{28,20},{1,9},{5... | collective-permute-start | bytes 3609608 | tf_op jit(solution)/shard_map/ppermute | solution.py:52
  343.8 53.3 %collective-permute-start.2 = (f32[1504,200]{0,1:T(8,128)S(1)}, f32[1504,200]{0,1:T(8,128)S(1)}, u32[]{:S(2)}, u32[]{:S(2)}) collective-permute-start(f32[1504,200]{0,1:T(8,128)S(1)} %add.49), channel_id=1, source_target_pairs={{0,16},{4,20},{8,24},{12,28},{16,0},{20,4},{24,8},{28,12},{1,17},{... | collective-permute-start | bytes 3609608 | tf_op jit(solution)/shard_map/ppermute | solution.py:52
  402.8 27.7 %copy-start.2 = (u32[32]{0:T(128)S(1)}, u32[32]{0:T(128)}, u32[]{:S(2)}) copy-start(u32[32]{0:T(128)} %constant.44) | copy-start | bytes 388
  428.5 46.9 %collective-permute-start.3 = (f32[2500,18]{0,1:T(8,128)S(1)}, f32[2500,18]{0,1:T(8,128)S(1)}, u32[]{:S(2)}, u32[]{:S(2)}) collective-permute-start(f32[2500,18]{0,1:T(8,128)S(1)} %slice), channel_id=1, source_target_pairs={{0,1},{1,2},{2,3},{4,5},{5,6},{6,7},{8,9},{9,10},{10,11},{12,13},{... | collective-permute-start | bytes 540008
Sparse Core Ops, SparseCore 0:
  86.3 23.7 all-gather.5
  130.9 82.0 all-gather.7
  217.9 55.3 all-reduce.5
